TPU v7x, 32 devices: a whole 2x2x4 slice. The times are simulated.
32 devices in a mesh: rep: 1, r: 4 (over z), s: 8 (over x, y, core).
Axes of the slice: x: 2, y: 2, z: 4, core: 2. Of those that a mesh axis runs over, the one named last changes fastest.
Arguments:
- x: bfloat16 [32, 4096, 640], P(('rep', 'r', 's'))
- dy: bfloat16 [32, 4096, 640], P(('rep', 'r', 's'))
- w_gate: bfloat16 [2, 640, 1792], P(None, 's')
- w_up: bfloat16 [2, 640, 1792], P(None, 's')
- w_down: bfloat16 [2, 1792, 640], P(None, 's')
- m_w_gate: float32 [2, 640, 1792], P(None, 's')
- m_w_up: float32 [2, 640, 1792], P(None, 's')
- m_w_down: float32 [2, 1792, 640], P(None, 's')
- v_w_gate: float32 [2, 640, 1792], P(None, 's')
- v_w_up: float32 [2, 640, 1792], P(None, 's')
- v_w_down: float32 [2, 1792, 640], P(None, 's')
Outputs:
- output 1: bfloat16 [2, 640, 1792], P('rep', 's')
- output 2: bfloat16 [2, 640, 1792], P('rep', 's')
- output 3: bfloat16 [2, 1792, 640], P('rep', 's')
- output 4: float32 [2, 640, 1792], P('rep', 's')
- output 5: float32 [2, 640, 1792], P('rep', 's')
- output 6: float32 [2, 1792, 640], P('rep', 's')
- output 7: float32 [2, 640, 1792], P('rep', 's')
- output 8: float32 [2, 640, 1792], P('rep', 's')
- output 9: float32 [2, 1792, 640], P('rep', 's')
All inputs are finite; a program needn't handle non-finite values.
Results may differ from a plain program's by a relative error of at most 0.02.
Values are sent between devices in bfloat16 or wider.
A program may use at most 2 GiB of HBM per device.

v0:
```python
import jax
import jax.numpy as jnp
from jax import lax
from jax.sharding import PartitionSpec as P

NAMES = ("w_gate", "w_up", "w_down")


def matmul(a, w):
    return jnp.dot(a, w, preferred_element_type=jnp.float32).astype(jnp.bfloat16)


def normed(h):
    wide = h.astype(jnp.float32)
    scale = lax.rsqrt(jnp.mean(wide**2, -1, keepdims=True) + 1e-6)
    return (wide * scale).astype(jnp.bfloat16)


def layer(h, w):
    a = normed(h)
    gate = jnp.dot(a, w["w_gate"], preferred_element_type=jnp.float32)
    up = jnp.dot(a, w["w_up"], preferred_element_type=jnp.float32)
    return h + matmul((jax.nn.silu(gate) * up).astype(jnp.bfloat16), w["w_down"])


def adamw(w, m, v, g):
    m = 0.9 * m + 0.1 * g
    v = 0.95 * v + 0.05 * g * g
    step = m * lax.rsqrt(v + 1e-8) + 0.1 * w
    return (w - 0.02 * step).astype(jnp.bfloat16), m, v


def solution(mesh):
    def fetched(weights, number):
        return {name: lax.all_gather(w[number], "s", axis=0, tiled=True) for name, w in zip(NAMES, weights, strict=True)}

    def summed(term):
        return lax.psum(lax.psum_scatter(term, "s", scatter_dimension=0, tiled=True), "r")

    def step(x, dy, *arrays):
        weights, m, v = (arrays[i : i + 3] for i in (0, 3, 6))
        layers = weights[0].shape[0]
        h, kept = x[0], []
        for number in range(layers):
            kept.append(h)
            h = layer(h, fetched(weights, number))
        by_h, mine = dy[0], [None] * layers
        for number in reversed(range(layers)):
            _, back = jax.vjp(lambda w, h: layer(h, w), fetched(weights, number), kept[number])
            by_w, by_h = back(by_h)
            mine[number] = [summed(by_w[name]) for name in NAMES]
        gradients = [jnp.stack([mine[number][i] for number in range(layers)]).astype(jnp.float32) for i in range(3)]
        new = [adamw(w.astype(jnp.float32), m, v, g) for w, m, v, g in zip(weights, m, v, gradients, strict=True)]
        return tuple(one[which] for which in range(3) for one in new)

    states, cut = P(("rep", "r", "s"), None, None), P(None, "s", None)
    return jax.shard_map(
        step,
        mesh=mesh,
        in_specs=(states, states) + (cut,) * 9,
        out_specs=(P("rep", "s", None),) * 9,
        check_vma=False,
    )
```

profile of v0, /device:TPU:0, one launch (start us, length us, event | category | flops | bytes accessed | tf_op | source)
XLA Modules:
  0.0 673.3 jit_solution(17567508016700012853)
XLA Ops:
  7.2 0.0 all-gather.13.cloned.1.call-start
  7.2 1.9 fusion.97
  9.1 0.0 all-gather.13.cloned.1.call-update
  9.1 0.0 all-gather.15.cloned.1.call-start
  9.2 1.9 fusion.96
  11.1 0.0 all-gather.15.cloned.1.call-update
  11.1 0.0 all-gather.17.cloned.1.call-start
  11.2 1.9 fusion.95
  13.1 0.0 all-gather.17.cloned.1.call-update
  13.1 0.0 all-gather.21.cloned.1.call-start
  13.1 0.5 all-gather.21.cloned.1.call-update
  13.7 0.0 all-gather.23.cloned.1.call-start
  13.7 0.5 all-gather.23.cloned.1.call-update
  14.2 0.0 all-gather.19.cloned.1.call-start
  14.3 0.5 all-gather.19.cloned.1.call-update
  14.8 0.0 reduce-scatter.9.cloned.1.call-start
  14.9 7.9 %copy.20 = bf16[1,4096,640]{1,2,0:T(8,128)(2,1)} copy(bf16[1,4096,640]{2,1,0:T(8,128)(2,1)} %param.11) | data formatting | bytes 10485760 | tf_op args[0]
  22.7 3.6 fusion.15
  26.4 0.0 copy-start.13
  26.4 8.0 %copy.21 = bf16[1,4096,640]{1,2,0:T(8,128)(2,1)} copy(bf16[1,4096,640]{2,1,0:T(8,128)(2,1)} %param.12) | data formatting | bytes 10485760 | tf_op args[1]
  34.4 7.2 %all-gather.13.cloned.1.call-done = bf16[1,640,1792]{2,1,0:T(8,128)(2,1)} async-done(((bf16[1,80,1792]{2,1,0:T(8,128)(2,1)}), bf16[1,640,1792]{2,1,0:T(8,128)(2,1)}) %all-gather.13.cloned.1.call-update) | async-done | bytes 2293776 | tf_op jit(solution)/shard_map/all_gather | solution.py:35
  41.6 19.5 %fusion.40 = f32[4096,1792]{1,0:T(8,128)} fusion(bf16[1,4096,640]{1,2,0:T(8,128)(2,1)} %copy.20, f32[4096]{0:T(1024)S(1)} %add_rsqrt_fusion, bf16[1,640,1792]{2,1,0:T(8,128)(2,1)} %all-gather.13.cloned.1.call-done), kind=kOutput, calls=%fused_computation.52 | convolution fusion | flops 9403105280 | bytes 36913152 | tf_op jit(solution)/shard_map/dot_general | solution.py:21
  61.1 11.3 %all-gather.15.cloned.1.call-done = bf16[1,640,1792]{2,1,0:T(8,128)(2,1)} async-done(((bf16[1,80,1792]{2,1,0:T(8,128)(2,1)}), bf16[1,640,1792]{2,1,0:T(8,128)(2,1)}) %all-gather.15.cloned.1.call-update) | async-done | bytes 2293776 | tf_op jit(solution)/shard_map/all_gather | solution.py:35
  72.4 33.1 %multiply_convert_fusion.1 = (bf16[4096,1792]{1,0:T(8,128)(2,1)}, f32[4096,1792]{1,0:T(8,128)}) fusion(f32[4096,1792]{1,0:T(8,128)} %fusion.40, bf16[1,640,1792]{2,1,0:T(8,128)(2,1)} %all-gather.15.cloned.1.call-done, bf16[1,4096,640]{1,2,0:T(8,128)(2,1)} %copy.20, f32[4096]{0:T(1024)S(1)} %add_rsqrt_fusion), kind=kOutput, calls=%fused_computation.17 | convolution fusion | flops 9447145472 | bytes 80953344 | tf_op jit(solution)/shard_map/dot_general | solution.py:22
  105.5 16.8 %fusion.19 = (f32[4096]{0:T(1024)S(1)}, bf16[4096,640]{0,1:T(8,128)(2,1)}) fusion(bf16[4096,1792]{1,0:T(8,128)(2,1)} %get-tuple-element.30, bf16[1,1792,640]{2,1,0:T(8,128)(2,1)} %all-gather.17.cloned.1.call-done, bf16[1,4096,640]{1,2,0:T(8,128)(2,1)} %copy.20), kind=kOutput, calls=%fused_computation.37 | convolution fusion | flops 9408344064 | bytes 27475968 | tf_op jit(solution)/shard_map/dot_general | solution.py:10
  122.3 0.6 copy-done.11
  122.9 11.0 %all-gather.21.cloned.1.call-done = bf16[1,1792,640]{2,1,0:T(8,128)(2,1)} async-done(((bf16[1,224,640]{2,1,0:T(8,128)(2,1)}), bf16[1,1792,640]{2,1,0:T(8,128)(2,1)}) %all-gather.21.cloned.1.call-update) | async-done | bytes 2293776 | tf_op jit(solution)/shard_map/all_gather | solution.py:35
  133.9 17.4 %convolution_convert_fusion.1 = bf16[4096,1792]{1,0:T(8,128)(2,1)} fusion(bf16[1,4096,640]{2,1,0:T(8,128)(2,1)} %param.12, bf16[1,1792,640]{2,1,0:T(8,128)(2,1)} %all-gather.21.cloned.1.call-done), kind=kOutput, calls=%fused_computation.27 | convolution fusion | flops 9402580992 | bytes 22216704 | tf_op jit(solution)/shard_map/transpose(jvp())/dot_general | solution.py:10
  151.3 13.3 %all-gather.23.cloned.1.call-done = bf16[1,640,1792]{2,1,0:T(8,128)(2,1)} async-done(((bf16[1,80,1792]{2,1,0:T(8,128)(2,1)}), bf16[1,640,1792]{2,1,0:T(8,128)(2,1)}) %all-gather.23.cloned.1.call-update) | async-done | bytes 2293776 | tf_op jit(solution)/shard_map/all_gather | solution.py:35
  164.6 19.5 %fusion.32 = f32[4096,1792]{1,0:T(8,128)} fusion(bf16[4096,640]{0,1:T(8,128)(2,1)} %get-tuple-element.33, f32[4096]{0:T(1024)S(1)} %fusion.83, bf16[1,640,1792]{2,1,0:T(8,128)(2,1)} %all-gather.23.cloned.1.call-done), kind=kOutput, calls=%fused_computation.49 | convolution fusion | flops 9403105280 | bytes 36913152 | tf_op jit(solution)/shard_map/jvp()/dot_general | solution.py:22
  184.1 11.2 %all-gather.19.cloned.1.call-done = bf16[1,640,1792]{2,1,0:T(8,128)(2,1)} async-done(((bf16[1,80,1792]{2,1,0:T(8,128)(2,1)}), bf16[1,640,1792]{2,1,0:T(8,128)(2,1)}) %all-gather.19.cloned.1.call-update) | async-done | bytes 2293776 | tf_op jit(solution)/shard_map/all_gather | solution.py:35
  195.3 39.4 %fusion.2 = (bf16[4096,1792]{1,0:T(8,128)(2,1)}, f32[4096,1792]{1,0:T(8,128)}) fusion(f32[4096,1792]{1,0:T(8,128)} %fusion.32, bf16[4096,1792]{1,0:T(8,128)(2,1)} %convolution_convert_fusion.1, bf16[1,640,1792]{2,1,0:T(8,128)(2,1)} %all-gather.19.cloned.1.call-done, bf16[4096,640]{0,1:T(8,128)(2,1)} %get-tuple-element.33, f32[4096]{0:T(1024)S(1)} %fusion.83), kind=kOutput, calls=%fused_computation.8 | convolution fusion | flops 9491185664 | bytes 95633408 | tf_op jit(solution)/shard_map/jvp()/dot_general | solution.py:21
  234.6 15.5 %fusion.42 = bf16[640,1792]{1,0:T(8,128)(2,1)} fusion(bf16[4096,1792]{1,0:T(8,128)(2,1)} %get-tuple-element.34, bf16[4096,640]{0,1:T(8,128)(2,1)} %get-tuple-element.33, f32[4096]{0:T(1024)S(1)} %fusion.83), kind=kOutput, calls=%fused_computation.53 | convolution fusion | flops 9403105280 | bytes 22233088 | tf_op jit(solution)/shard_map/transpose(jvp())/dot_general | solution.py:21
  250.1 0.0 reduce-scatter.9.cloned.1.call-update
  250.1 0.0 reduce-scatter.7.cloned.1.call-start
  250.2 22.0 %fusion.22 = bf16[4096,640]{0,1:T(8,128)(2,1)} fusion(bf16[4096,1792]{1,0:T(8,128)(2,1)} %convolution_convert_fusion.1, bf16[1,640,1792]{2,1,0:T(8,128)(2,1)S(1)} %copy-done.16, f32[4096,1792]{1,0:T(8,128)} %get-tuple-element.35), kind=kOutput, calls=%fused_computation.40 | convolution fusion | flops 9441902592 | bytes 51576832 | tf_op jit(solution)/shard_map/transpose(jvp())/dot_general | solution.py:22
  272.3 26.8 %fusion.21 = (f32[4096]{0:T(1024)S(1)}, bf16[4096,640]{0,1:T(8,128)(2,1)}) fusion(bf16[4096,640]{0,1:T(8,128)(2,1)S(1)} %bitcast.69, bf16[4096,640]{0,1:T(8,128)(2,1)} %fusion.22, bf16[4096,1792]{1,0:T(8,128)(2,1)} %get-tuple-element.34, bf16[1,640,1792]{2,1,0:T(8,128)(2,1)S(1)} %copy-done.17), kind=kOutput, calls=%fused_computation.39 | convolution fusion | flops 9408344064 | bytes 32718848 | tf_op jit(solution)/shard_map/transpose(jvp())/dot_general | solution.py:21
  299.1 12.0 %fusion.25 = bf16[4096,640]{0,1:T(8,128)(2,1)} fusion(bf16[4096,640]{0,1:T(8,128)(2,1)} %get-tuple-element.33, bf16[4096,640]{0,1:T(8,128)(2,1)} %get-tuple-element.37, bf16[1,4096,640]{1,2,0:T(8,128)(2,1)} %copy.21, f32[4096]{0:T(1024)S(1)} %multiply_multiply_fusion.3, f32[4096]{0:T(1024)S(1)} %fusion.83), kind=kLoop, calls=%fused_computation.45 | loop fusion | flops 18350080 | bytes 21004288 | tf_op jit(solution)/shard_map/transpose(jvp())/add_any | solution.py:14
  311.1 18.8 %convolution_convert_fusion = bf16[4096,1792]{1,0:T(8,128)(2,1)} fusion(bf16[4096,640]{0,1:T(8,128)(2,1)} %fusion.25, bf16[1,1792,640]{2,1,0:T(8,128)(2,1)S(1)} %copy-done.15), kind=kOutput, calls=%fused_computation.26 | convolution fusion | flops 9402580992 | bytes 22216704 | tf_op jit(solution)/shard_map/transpose(jvp())/dot_general | solution.py:10
  329.9 29.5 %fusion.54 = bf16[640,1792]{1,0:T(8,128)(2,1)} fusion(f32[4096,1792]{1,0:T(8,128)} %fusion.40, f32[4096,1792]{1,0:T(8,128)} %get-tuple-element.31, bf16[4096,1792]{1,0:T(8,128)(2,1)} %convolution_convert_fusion, bf16[1,4096,640]{1,2,0:T(8,128)(2,1)} %copy.20, f32[4096]{0:T(1024)S(1)} %copy-done.14), kind=kOutput, calls=%fused_computation.58 | convolution fusion | flops 9484992512 | bytes 80953344 | tf_op jit(solution)/shard_map/transpose(jvp())/dot_general | solution.py:21
  359.4 0.0 reduce-scatter.7.cloned.1.call-update
  359.4 0.0 reduce-scatter.13.cloned.1.call-start
  359.5 23.1 %fusion.48 = bf16[640,1792]{1,0:T(8,128)(2,1)} fusion(bf16[4096,1792]{1,0:T(8,128)(2,1)} %convolution_convert_fusion.1, bf16[4096,640]{0,1:T(8,128)(2,1)} %get-tuple-element.33, f32[4096]{0:T(1024)S(1)} %fusion.83, f32[4096,1792]{1,0:T(8,128)} %get-tuple-element.35), kind=kOutput, calls=%fused_computation.55 | convolution fusion | flops 9448292352 | bytes 51593216 | tf_op jit(solution)/shard_map/transpose(jvp())/dot_general | solution.py:22
  382.6 0.0 reduce-scatter.13.cloned.1.call-update
  382.6 0.0 reduce-scatter.11.cloned.1.call-start
  382.7 22.9 %fusion.51 = bf16[640,1792]{1,0:T(8,128)(2,1)} fusion(bf16[4096,1792]{1,0:T(8,128)(2,1)} %convolution_convert_fusion, f32[4096,1792]{1,0:T(8,128)} %fusion.40, bf16[1,4096,640]{1,2,0:T(8,128)(2,1)} %copy.20, f32[4096]{0:T(1024)S(1)} %copy-done.14), kind=kOutput, calls=%fused_computation.56 | convolution fusion | flops 9448292352 | bytes 51593216 | tf_op jit(solution)/shard_map/transpose(jvp())/dot_general | solution.py:22
  405.6 0.0 reduce-scatter.11.cloned.1.call-update
  405.6 0.0 reduce-scatter.17.cloned.1.call-start
  405.6 25.6 %fusion.45 = bf16[1792,640]{1,0:T(8,128)(2,1)} fusion(bf16[1,4096,640]{2,1,0:T(8,128)(2,1)} %param.12, f32[4096,1792]{1,0:T(8,128)} %fusion.32, f32[4096,1792]{1,0:T(8,128)} %get-tuple-element.35), kind=kOutput, calls=%fused_computation.54 | convolution fusion | flops 9440428032 | bytes 66256896 | tf_op jit(solution)/shard_map/transpose(jvp())/dot_general | solution.py:10
  431.2 0.0 reduce-scatter.17.cloned.1.call-update
  431.2 0.0 reduce-scatter.15.cloned.1.call-start
  431.3 17.4 %convolution_convert_fusion.4 = bf16[1792,640]{1,0:T(8,128)(2,1)} fusion(bf16[4096,1792]{1,0:T(8,128)(2,1)} %get-tuple-element.30, bf16[4096,640]{0,1:T(8,128)(2,1)} %fusion.25), kind=kOutput, calls=%fused_computation.57 | convolution fusion | flops 9396387840 | bytes 22216704 | tf_op jit(solution)/shard_map/transpose(jvp())/dot_general | solution.py:10
  448.7 0.0 reduce-scatter.15.cloned.1.call-update
  448.8 0.3 all-reduce.3.cloned.1.call-start
  449.1 0.0 reduce-scatter.9.cloned.1.call-done
  449.1 0.0 reduce-scatter.7.cloned.1.call-done
  449.2 0.0 reduce-scatter.13.cloned.1.call-done
  449.2 42.6 %reduce-scatter.11.cloned.1.call-done = bf16[80,1792]{1,0:T(8,128)(2,1)} async-done(((bf16[640,1792]{1,0:T(8,128)(2,1)}), bf16[80,1792]{1,0:T(8,128)(2,1)}) %reduce-scatter.11.cloned.1.call-update) | async-done | bytes 286736 | tf_op jit(solution)/shard_map/reduce_scatter | solution.py:38
  491.8 45.2 %reduce-scatter.17.cloned.1.call-done = bf16[224,640]{1,0:T(8,128)(2,1)} async-done(((bf16[1792,640]{1,0:T(8,128)(2,1)}), bf16[224,640]{1,0:T(8,128)(2,1)}) %reduce-scatter.17.cloned.1.call-update) | async-done | bytes 286736 | tf_op jit(solution)/shard_map/reduce_scatter | solution.py:38
  537.0 45.1 %reduce-scatter.15.cloned.1.call-done = bf16[224,640]{1,0:T(8,128)(2,1)} async-done(((bf16[1792,640]{1,0:T(8,128)(2,1)}), bf16[224,640]{1,0:T(8,128)(2,1)}) %reduce-scatter.15.cloned.1.call-update) | async-done | bytes 286736 | tf_op jit(solution)/shard_map/reduce_scatter | solution.py:38
  582.1 0.0 all-reduce.3.cloned.1.call-update
  582.1 77.0 %all-reduce.3.cloned.1.call-done = (bf16[1,80,1792]{2,1,0:T(8,128)(2,1)}, bf16[1,80,1792]{2,1,0:T(8,128)(2,1)}, bf16[1,80,1792]{2,1,0:T(8,128)(2,1)}, bf16[1,80,...) async-done(((bf16[1,80,1792]{2,1,0:T(8,128)(2,1)}, bf16[1,80,1792]{2,1,0:T(8,128)(2,1)}, bf16[1,80,1792]{2,1,0:T(8,128)(2,1)}, ...) | async-done | bytes 1720336 | tf_op jit(solution)/shard_map/psum | solution.py:38
  659.2 3.8 fusion.78
  663.1 3.2 fusion.70
  (43 shorter events, 0.1 us)
Async XLA Ops:
  7.2 34.4 %all-gather.13.cloned.1.call-start = ((), (), s32[]{:S(2)}) async-start(), calls=%async_computation.12 | async-start | bytes 2580480 | tf_op jit(solution)/shard_map/all_gather | solution.py:35
  9.1 63.3 %all-gather.15.cloned.1.call-start = ((), (), s32[]{:S(2)}) async-start(), calls=%async_computation.13 | async-start | bytes 2580480 | tf_op jit(solution)/shard_map/all_gather | solution.py:35
  11.1 94.4 %all-gather.17.cloned.1.call-start = ((), (), s32[]{:S(2)}) async-start(), calls=%async_computation.14 | async-start | bytes 2580480 | tf_op jit(solution)/shard_map/all_gather | solution.py:35
  13.1 120.8 %all-gather.21.cloned.1.call-start = ((), (), s32[]{:S(2)}) async-start(), calls=%async_computation.16 | async-start | bytes 2580480 | tf_op jit(solution)/shard_map/all_gather | solution.py:35
  13.7 150.9 %all-gather.23.cloned.1.call-start = ((), (), s32[]{:S(2)}) async-start(), calls=%async_computation.17 | async-start | bytes 2580480 | tf_op jit(solution)/shard_map/all_gather | solution.py:35
  14.2 181.0 %all-gather.19.cloned.1.call-start = ((), (), s32[]{:S(2)}) async-start(), calls=%async_computation.15 | async-start | bytes 2580480 | tf_op jit(solution)/shard_map/all_gather | solution.py:35
  14.8 434.3 %reduce-scatter.9.cloned.1.call-start = ((), (), s32[]{:S(2)}) async-start(), calls=%async_computation.7 | async-start | bytes 2580480 | tf_op jit(solution)/shard_map/reduce_scatter | solution.py:38
  26.4 46.0 %copy-start.13 = (f32[4096]{0:T(1024)}, f32[4096]{0:T(1024)S(1)}, u32[]{:S(2)}) copy-start(f32[4096]{0:T(1024)S(1)} %add_rsqrt_fusion) | copy-start | bytes 49156
  122.3 0.6 copy-start.11
  234.6 15.6 %copy-start.16 = (bf16[1,640,1792]{2,1,0:T(8,128)(2,1)S(1)}, bf16[1,640,1792]{2,1,0:T(8,128)(2,1)}, u32[]{:S(2)}) copy-start(bf16[1,640,1792]{2,1,0:T(8,128)(2,1)} %all-gather.23.cloned.1.call-done) | copy-start | bytes 6881284
  234.6 37.6 %slice-start = ((s8[5242880]{0:T(1024)(128)(4,1)}), s8[1048576]{0:T(1024)(128)(4,1)S(1)}, s32[]{:S(2)}) async-start(s8[5242880]{0:T(1024)(128)(4,1)} %bitcast.68), calls=%async_computation.19 | async-start | bytes 2097152
  250.1 199.0 %reduce-scatter.7.cloned.1.call-start = ((), (), s32[]{:S(2)}) async-start(), calls=%async_computation.6 | async-start | bytes 2580480 | tf_op jit(solution)/shard_map/reduce_scatter | solution.py:38
  250.2 22.1 %slice-start.1 = ((s8[5242880]{0:T(1024)(128)(4,1)}), s8[4194304]{0:T(1024)(128)(4,1)S(1)}, s32[]{:S(2)}) async-start(s8[5242880]{0:T(1024)(128)(4,1)} %bitcast.68), calls=%async_computation.20 | async-start | bytes 8388608
  250.2 22.1 %copy-start.17 = (bf16[1,640,1792]{2,1,0:T(8,128)(2,1)S(1)}, bf16[1,640,1792]{2,1,0:T(8,128)(2,1)}, u32[]{:S(2)}) copy-start(bf16[1,640,1792]{2,1,0:T(8,128)(2,1)} %all-gather.19.cloned.1.call-done) | copy-start | bytes 6881284
  272.3 26.8 %copy-start.12 = (f32[4096]{0:T(1024)S(1)}, f32[4096]{0:T(1024)}, u32[]{:S(2)}) copy-start(f32[4096]{0:T(1024)} %copy-done.11) | copy-start | bytes 49156
  299.1 12.0 %copy-start.15 = (bf16[1,1792,640]{2,1,0:T(8,128)(2,1)S(1)}, bf16[1,1792,640]{2,1,0:T(8,128)(2,1)}, u32[]{:S(2)}) copy-start(bf16[1,1792,640]{2,1,0:T(8,128)(2,1)} %all-gather.17.cloned.1.call-done) | copy-start | bytes 6881284
  311.1 18.8 %copy-start.14 = (f32[4096]{0:T(1024)S(1)}, f32[4096]{0:T(1024)}, u32[]{:S(2)}) copy-start(f32[4096]{0:T(1024)} %copy-done.13) | copy-start | bytes 49156
  359.4 89.8 %reduce-scatter.13.cloned.1.call-start = ((), (), s32[]{:S(2)}) async-start(), calls=%async_computation.9 | async-start | bytes 2580480 | tf_op jit(solution)/shard_map/reduce_scatter | solution.py:38
  382.6 109.2 %reduce-scatter.11.cloned.1.call-start = ((), (), s32[]{:S(2)}) async-start(), calls=%async_computation.8 | async-start | bytes 2580480 | tf_op jit(solution)/shard_map/reduce_scatter | solution.py:38
  405.6 131.4 %reduce-scatter.17.cloned.1.call-start = ((), (), s32[]{:S(2)}) async-start(), calls=%async_computation.11 | async-start | bytes 2580480 | tf_op jit(solution)/shard_map/reduce_scatter | solution.py:38
  431.2 227.9 %copy-start = (bf16[2,224,640]{2,1,0:T(8,128)(2,1)S(1)}, bf16[2,224,640]{2,1,0:T(8,128)(2,1)}, u32[]{:S(2)}) copy-start(bf16[2,224,640]{2,1,0:T(8,128)(2,1)} %param.15) | copy-start | bytes 1720324
  431.2 150.8 %reduce-scatter.15.cloned.1.call-start = ((), (), s32[]{:S(2)}) async-start(), calls=%async_computation.10 | async-start | bytes 2580480 | tf_op jit(solution)/shard_map/reduce_scatter | solution.py:38
  448.7 214.3 %copy-start.1 = (bf16[2,80,1792]{2,1,0:T(8,128)(2,1)S(1)}, bf16[2,80,1792]{2,1,0:T(8,128)(2,1)}, u32[]{:S(2)}) copy-start(bf16[2,80,1792]{2,1,0:T(8,128)(2,1)} %param.13) | copy-start | bytes 1720324
  448.7 214.3 %copy-start.2 = (bf16[2,80,1792]{2,1,0:T(8,128)(2,1)S(1)}, bf16[2,80,1792]{2,1,0:T(8,128)(2,1)}, u32[]{:S(2)}) copy-start(bf16[2,80,1792]{2,1,0:T(8,128)(2,1)} %param.14) | copy-start | bytes 1720324
  448.7 214.3 %copy-start.3 = (f32[2,80,1792]{2,1,0:T(8,128)S(1)}, f32[2,80,1792]{2,1,0:T(8,128)}, u32[]{:S(2)}) copy-start(f32[2,80,1792]{2,1,0:T(8,128)} %param.19) | copy-start | bytes 3440644
  448.8 210.4 %all-reduce.3.cloned.1.call-start = ((), (), s32[]{:S(2)}) async-start(), calls=%async_computation.18 | async-start | bytes 3440640 | tf_op jit(solution)/shard_map/psum | solution.py:38
  659.1 3.9 copy-start.4
  659.1 3.9 copy-start.5
  659.1 3.9 copy-start.6
  659.1 3.9 copy-start.7
  659.2 3.9 copy-start.8
  659.2 3.9 copy-start.9
  659.2 3.9 copy-start.10
Sparse Core Ops, SparseCore 0:
  10.4 31.0 all-gather.12
  44.0 28.3 all-gather.14
  74.9 28.3 all-gather.16
  105.5 28.3 all-gather.20
  136.2 28.3 all-gather.22
  166.9 28.3 all-gather.18
  250.2 41.8 reduce-scatter.8
  359.5 41.8 reduce-scatter.6
  404.8 41.8 reduce-scatter.12
  449.9 41.8 reduce-scatter.10
  495.1 41.8 reduce-scatter.16
  540.2 41.8 reduce-scatter.14
  584.9 74.1 all-reduce.2
where the time goes:
time: 680 us; the launch traced here: 673 us
  matrix products  347 us (51%)
  waiting for transfers between devices  266 us (39%)
  other arithmetic  22.6 us (3%)
  local copies, waits for them, and re-layouts  22.2 us (3%)
  between operations  14.6 us (2%)
    reduce_scatter x6, waiting for transfers between devices, summed(): lax.psum_scatter(term, 's', scatter_dimension=0, tiled=True)  133 us
    dot_general x5, matrix products, layer(): gate = jnp.dot(a, w['w_gate'], preferred_element_type=jnp.float32)  131 us
    dot_general x5, matrix products, layer(): up = jnp.dot(a, w['w_up'], preferred_element_type=jnp.float32)  121 us
    dot_general x5, matrix products, matmul(): jnp.dot(a, w, preferred_element_type=jnp.float32).astype(jnp.bfloat16)  96 us
    psum x1, waiting for transfers between devices, summed(): lax.psum(lax.psum_scatter(term, 's', scatter_dimension=0, tiled=True), 'r')  77 us
    all_gather x6, waiting for transfers between devices, fetched(): lax.all_gather(w[number], 's', axis=0, tiled=True)  54 us
    unnamed x42, local copies, waits for them, and re-layouts  16.5 us
  transfers between devices with their start and end apart: 13, of which 9 were waited for; matrix products, arithmetic and copies ran while one was open for 49% of the time, Pallas kernels for 0%

commit v1 on v0

v1 whole, which is shorter than its diff:
```python
import functools

import jax
import jax.numpy as jnp
from jax import lax
from jax.experimental import pallas as pl
from jax.experimental.pallas import tpu as pltpu
from jax.sharding import PartitionSpec as P

NAMES = ("w_gate", "w_up", "w_down")
F32, BF16 = jnp.float32, jnp.bfloat16
NN = (((1,), (0,)), ((), ()))
NT = (((1,), (1,)), ((), ()))


def dot(a, b, dims=NN):
    return lax.dot_general(a, b, dims, preferred_element_type=F32)


def normed(h):
    wide = h.astype(F32)
    scale = lax.rsqrt(jnp.mean(wide * wide, -1, keepdims=True) + 1e-6)
    return wide, scale


def sigmoid(g):
    return 0.5 * jnp.tanh(0.5 * g) + 0.5


def first_forward(x_ref, wg_ref, wu_ref, wd_ref, h_ref, g_ref, u_ref, hid_ref, *, cut):
    wide, scale = normed(x_ref[...])
    a = (wide * scale).astype(BF16)
    ff = wg_ref.shape[1]
    for j in range(0, ff, cut):
        g = dot(a, wg_ref[:, j : j + cut])
        u = dot(a, wu_ref[:, j : j + cut])
        g_ref[:, j : j + cut] = g
        u_ref[:, j : j + cut] = u
        hid_ref[:, j : j + cut] = (g * sigmoid(g) * u).astype(BF16)
    y = dot(hid_ref[...], wd_ref[...]).astype(BF16)
    h_ref[...] = x_ref[...] + y


def back_through(dh, wide, scale, da):
    inner = jnp.mean(da * wide, -1, keepdims=True)
    by_norm = scale * da - wide * (scale * scale * scale * inner)
    return dh + by_norm.astype(BF16)


def last_layer(h_ref, dy_ref, wg_ref, wu_ref, wd_ref, dh_ref, og_ref, ou_ref, od_ref, acc_g, acc_u, acc_d, dg_ref, du_ref, *, cut):
    i, n = pl.program_id(0), pl.num_programs(0)

    @pl.when(i == 0)
    def _():
        acc_g[...] = jnp.zeros_like(acc_g)
        acc_u[...] = jnp.zeros_like(acc_u)
        acc_d[...] = jnp.zeros_like(acc_d)

    wide, scale = normed(h_ref[...])
    a = (wide * scale).astype(BF16)
    dy = dy_ref[...]
    a_t, dy_t = a.T, dy.T
    ff = wg_ref.shape[1]
    for j in range(0, ff, cut):
        at = slice(j, j + cut)
        g = dot(a, wg_ref[:, at])
        u = dot(a, wu_ref[:, at])
        dhid = dot(dy, wd_ref[at, :], NT).astype(BF16).astype(F32)
        sig = sigmoid(g)
        s = g * sig
        hid = (s * u).astype(BF16)
        du = (dhid * s).astype(BF16)
        dg = (dhid * u * (sig * (1.0 + g - s))).astype(BF16)
        dg_ref[:, at] = dg
        du_ref[:, at] = du
        acc_d[:, at] += dot(dy_t, hid)
        acc_g[:, at] += dot(a_t, dg)
        acc_u[:, at] += dot(a_t, du)
    da = (dot(dg_ref[...], wg_ref[...], NT) + dot(du_ref[...], wu_ref[...], NT)).astype(BF16).astype(F32)
    dh_ref[...] = back_through(dy, wide, scale, da)

    @pl.when(i == n - 1)
    def _():
        og_ref[...] = acc_g[...].astype(BF16)
        ou_ref[...] = acc_u[...].astype(BF16)
        od_ref[...] = acc_d[...].T.astype(BF16)


def first_back(x_ref, dh_ref, g_ref, u_ref, wd_ref, og_ref, ou_ref, od_ref, acc_g, acc_u, acc_d, *, cut):
    i, n = pl.program_id(0), pl.num_programs(0)

    @pl.when(i == 0)
    def _():
        acc_g[...] = jnp.zeros_like(acc_g)
        acc_u[...] = jnp.zeros_like(acc_u)
        acc_d[...] = jnp.zeros_like(acc_d)

    wide, scale = normed(x_ref[...])
    a_t = (wide * scale).astype(BF16).T
    dh = dh_ref[...]
    dh_t = dh.T
    ff = g_ref.shape[1]
    for j in range(0, ff, cut):
        at = slice(j, j + cut)
        g, u = g_ref[:, at], u_ref[:, at]
        dhid = dot(dh, wd_ref[at, :], NT).astype(BF16).astype(F32)
        sig = sigmoid(g)
        s = g * sig
        hid = (s * u).astype(BF16)
        du = (dhid * s).astype(BF16)
        dg = (dhid * u * (sig * (1.0 + g - s))).astype(BF16)
        acc_d[:, at] += dot(dh_t, hid)
        acc_g[:, at] += dot(a_t, dg)
        acc_u[:, at] += dot(a_t, du)

    @pl.when(i == n - 1)
    def _():
        og_ref[...] = acc_g[...].astype(BF16)
        ou_ref[...] = acc_u[...].astype(BF16)
        od_ref[...] = acc_d[...].T.astype(BF16)


def whole(shape):
    return pl.BlockSpec(shape, lambda i: (0,) * len(shape), pipeline_mode=pl.Buffered(1))


def rows(n, width):
    return pl.BlockSpec((n, width), lambda i: (i, 0))


def struct(shape, dtype):
    return jax.ShapeDtypeStruct(shape, dtype)


def adamw(w, m, v, g):
    m = 0.9 * m + 0.1 * g
    v = 0.95 * v + 0.05 * g * g
    step = m * lax.rsqrt(v + 1e-8) + 0.1 * w
    return (w - 0.02 * step).astype(BF16), m, v


def solution(mesh):
    def fetched(weights, number):
        return [lax.all_gather(w[number], "s", axis=0, tiled=True) for w in weights]

    def summed(term):
        return lax.psum(lax.psum_scatter(term, "s", scatter_dimension=0, tiled=True), "r")

    def step(x, dy, *arrays):
        weights, m, v = (arrays[i : i + 3] for i in (0, 3, 6))
        x, dy = x[0], dy[0]
        tokens, d = x.shape
        ff = weights[0].shape[2]
        cut, tile = 256, 512
        params = pltpu.CompilerParams(vmem_limit_bytes=62 * 2**20, dimension_semantics=("arbitrary",))
        one = 2 * tokens * d * ff
        by0, by1 = fetched(weights, 0), fetched(weights, 1)
        h, g, u = pl.pallas_call(
            functools.partial(first_forward, cut=cut),
            grid=(tokens // tile,),
            in_specs=[rows(tile, d), whole((d, ff)), whole((d, ff)), whole((ff, d))],
            out_specs=[rows(tile, d), rows(tile, ff), rows(tile, ff)],
            out_shape=[struct((tokens, d), BF16), struct((tokens, ff), F32), struct((tokens, ff), F32)],
            scratch_shapes=[pltpu.VMEM((tile, ff), BF16)],
            compiler_params=params,
            cost_estimate=pl.CostEstimate(flops=3 * one, bytes_accessed=8 * tokens * ff, transcendentals=0),
            name="first_forward",
        )(x, *by0)
        grads = [struct((d, ff), BF16), struct((d, ff), BF16), struct((ff, d), BF16)]
        grad_specs = [whole((d, ff)), whole((d, ff)), whole((ff, d))]
        accs = [pltpu.VMEM((d, ff), F32)] * 3
        dh, *by_w1 = pl.pallas_call(
            functools.partial(last_layer, cut=cut),
            grid=(tokens // tile,),
            in_specs=[rows(tile, d), rows(tile, d), whole((d, ff)), whole((d, ff)), whole((ff, d))],
            out_specs=[rows(tile, d)] + grad_specs,
            out_shape=[struct((tokens, d), BF16)] + grads,
            scratch_shapes=accs + [pltpu.VMEM((tile, ff), BF16)] * 2,
            compiler_params=params,
            cost_estimate=pl.CostEstimate(flops=8 * one, bytes_accessed=8 * tokens * d, transcendentals=0),
            name="last_layer",
        )(h, dy, *by1)
        by_w0 = pl.pallas_call(
            functools.partial(first_back, cut=cut),
            grid=(tokens // tile,),
            in_specs=[rows(tile, d), rows(tile, d), rows(tile, ff), rows(tile, ff), whole((ff, d))],
            out_specs=grad_specs,
            out_shape=grads,
            scratch_shapes=accs,
            compiler_params=params,
            cost_estimate=pl.CostEstimate(flops=4 * one, bytes_accessed=8 * tokens * ff, transcendentals=0),
            name="first_back",
        )(x, dh, g, u, by0[2])
        mine = [[summed(t) for t in by_w] for by_w in (by_w0, by_w1)]
        gradients = [jnp.stack([a, b]).astype(F32) for a, b in zip(*mine)]
        new = [adamw(w.astype(F32), mm, vv, gg) for w, mm, vv, gg in zip(weights, m, v, gradients, strict=True)]
        return tuple(one[which] for which in range(3) for one in new)

    states, cut = P(("rep", "r", "s"), None, None), P(None, "s", None)
    return jax.shard_map(
        step,
        mesh=mesh,
        in_specs=(states, states) + (cut,) * 9,
        out_specs=(P("rep", "s", None),) * 9,
        check_vma=False,
    )
```

time: 680 us -> 733 us (1.078)
  matrix products: 347 us -> 0 us
  waiting for transfers between devices: 266 us -> 487 us
  Pallas kernels: 0 us -> 219 us
  local copies, waits for them, and re-layouts: 22.2 us -> 4.63 us
  other arithmetic: 22.6 us -> 7.27 us
    dot_general x15 -> x0, matrix products: 347 us -> none  [the longest x5 131 us: layer(): gate = jnp.dot(a, w['w_gate'], preferred_element_type=jnp.float32)]
    pallas_call x0 -> x3, Pallas kernels: none -> 219 us  [the longest x1 119 us: step(): pl.pallas_call(functools.partial(last_layer, cut=cut), grid=(tokens // ti...]
    reduce_scatter x6, waiting for transfers between devices: 133 us -> 264 us  [summed(): lax.psum_scatter(term, 's', scatter_dimension=0, tiled=True)]
    all_gather x6, waiting for transfers between devices: 54 us -> 140 us  [fetched(): return [lax.all_gather(w[number], 's', axis=0, tiled=True) for w in weights]]
    unnamed x42 -> x26, local copies, waits for them, and re-layouts: 16.5 us -> 0.99 us
    add_any x1 -> x0, other arithmetic: 12 us -> none  [normed(): wide = h.astype(jnp.float32)]
  transfers between devices with their start and end apart: 13 -> 13, of which waited for: 9 -> 12; matrix products, arithmetic and copies ran while one was open for 49% -> 0% of each run, Pallas kernels for 0% -> 6%
where the time goes in v1:
time: 733 us; the launch traced here: 732 us
  waiting for transfers between devices  487 us (66%)
  Pallas kernels  219 us (30%)
  between operations  14 us (2%)
    reduce_scatter x6, waiting for transfers between devices, summed(): lax.psum_scatter(term, 's', scatter_dimension=0, tiled=True)  264 us
    all_gather x6, waiting for transfers between devices, fetched(): return [lax.all_gather(w[number], 's', axis=0, tiled=True) for w in weights]  140 us
    pallas_call x1, Pallas kernels, step(): pl.pallas_call(functools.partial(last_layer, cut=cut), grid=(tokens // ti...  119 us
    psum x1, waiting for transfers between devices, summed(): lax.psum(lax.psum_scatter(term, 's', scatter_dimension=0, tiled=True), 'r')  77.1 us
    pallas_call x1, Pallas kernels, step(): pl.pallas_call(functools.partial(first_back, cut=cut), grid=(tokens // ti...  58.6 us
    pallas_call x1, Pallas kernels, step(): pl.pallas_call(functools.partial(first_forward, cut=cut), grid=(tokens //...  41.9 us
  transfers between devices with their start and end apart: 13, of which 12 were waited for; matrix products, arithmetic and copies ran while one was open for 0% of the time, Pallas kernels for 6%

profile of v1, /device:TPU:0, one launch (start us, length us, event | category | flops | bytes accessed | tf_op | source)
XLA Modules:
  0.0 732.3 jit_solution(5954822102806208782)
XLA Ops:
  7.2 0.0 copy-start.3
  7.2 0.0 all-gather.13.cloned.1.call-start
  7.2 1.9 fusion.23
  9.2 0.0 all-gather.13.cloned.1.call-update
  9.2 0.0 all-gather.15.cloned.1.call-start
  9.3 0.0 copy-done.3
  9.3 0.8 fusion.22
  10.1 0.0 all-gather.15.cloned.1.call-update
  10.1 0.0 all-gather.17.cloned.1.call-start
  10.2 0.1 copy-done
  10.3 0.9 fusion.21
  11.2 0.0 all-gather.17.cloned.1.call-update
  11.2 0.0 all-gather.19.cloned.1.call-start
  11.2 0.5 all-gather.19.cloned.1.call-update
  11.8 0.0 all-gather.21.cloned.1.call-start
  11.8 0.5 all-gather.21.cloned.1.call-update
  12.4 0.0 all-gather.23.cloned.1.call-start
  12.4 0.5 all-gather.23.cloned.1.call-update
  12.9 0.0 reduce-scatter.7.cloned.1.call-start
  13.0 28.6 %all-gather.13.cloned.1.call-done = bf16[1,640,1792]{2,1,0:T(8,128)(2,1)} async-done(((bf16[1,80,1792]{2,1,0:T(8,128)(2,1)}), bf16[1,640,1792]{2,1,0:T(8,128)(2,1)}) %all-gather.13.cloned.1.call-update) | async-done | bytes 2293776 | tf_op jit(solution)/shard_map/all_gather | solution.py:144
  41.6 30.8 %all-gather.15.cloned.1.call-done = bf16[1,640,1792]{2,1,0:T(8,128)(2,1)} async-done(((bf16[1,80,1792]{2,1,0:T(8,128)(2,1)}), bf16[1,640,1792]{2,1,0:T(8,128)(2,1)}) %all-gather.15.cloned.1.call-update) | async-done | bytes 2293776 | tf_op jit(solution)/shard_map/all_gather | solution.py:144
  72.4 30.8 %all-gather.17.cloned.1.call-done = bf16[1,1792,640]{2,1,0:T(8,128)(2,1)} async-done(((bf16[1,224,640]{2,1,0:T(8,128)(2,1)}), bf16[1,1792,640]{2,1,0:T(8,128)(2,1)}) %all-gather.17.cloned.1.call-update) | async-done | bytes 2293776 | tf_op jit(solution)/shard_map/all_gather | solution.py:144
  103.2 41.9 %first_forward.1 = (bf16[4096,640]{1,0:T(8,128)(2,1)}, f32[4096,1792]{1,0:T(8,128)}, f32[4096,1792]{1,0:T(8,128)}) custom-call(bf16[4096,640]{1,0:T(8,128)(2,1)} %bitcast.21, bf16[640,1792]{1,0:T(8,128)(2,1)} %bitcast.25, bf16[640,1792]{1,0:T(8,128)(2,1)} %bitcast.26, bf16[1792,640]{1,0:T(8,128)(2,1)} %bitcast.23), custom_call_target="tpu_custom_call" | custom-call | flops 28185722880 | bytes 58720256 | tf_op jit(solution)/shard_map/first_forward/pallas_call | solution.py:158
  145.2 19.4 %all-gather.21.cloned.1.call-done = bf16[1,640,1792]{2,1,0:T(8,128)(2,1)} async-done(((bf16[1,80,1792]{2,1,0:T(8,128)(2,1)}), bf16[1,640,1792]{2,1,0:T(8,128)(2,1)}) %all-gather.21.cloned.1.call-update) | async-done | bytes 2293776 | tf_op jit(solution)/shard_map/all_gather | solution.py:144
  164.6 30.7 %all-gather.23.cloned.1.call-done = bf16[1,1792,640]{2,1,0:T(8,128)(2,1)} async-done(((bf16[1,224,640]{2,1,0:T(8,128)(2,1)}), bf16[1,1792,640]{2,1,0:T(8,128)(2,1)}) %all-gather.23.cloned.1.call-update) | async-done | bytes 2293776 | tf_op jit(solution)/shard_map/all_gather | solution.py:144
  195.3 118.7 %last_layer.1 = (bf16[4096,640]{1,0:T(8,128)(2,1)}, bf16[640,1792]{1,0:T(8,128)(2,1)}, bf16[640,1792]{1,0:T(8,128)(2,1)}, bf16[1792,640]{1,0:T(8,128)(2,1)}) custom-call(bf16[4096,640]{1,0:T(8,128)(2,1)} %get-tuple-element.19.h_ref, bf16[4096,640]{1,0:T(8,128)(2,1)} %bitcast.20, bf16[640,1792]{1,0:T(8,128)(2,1)} %bitcast.27, bf16[640,1792]{1,0:T(8,128)(2,1)} %bitcast.28, ...), custom_call_target="tpu_custom_call" | custom-call | flops 75161927680 | bytes 20971520 | tf_op jit(solution)/shard_map/last_layer/pallas_call | solution.py:172
  314.0 58.6 %first_back.1 = (bf16[640,1792]{1,0:T(8,128)(2,1)}, bf16[640,1792]{1,0:T(8,128)(2,1)}, bf16[1792,640]{1,0:T(8,128)(2,1)}) custom-call(bf16[4096,640]{1,0:T(8,128)(2,1)} %bitcast.22, bf16[4096,640]{1,0:T(8,128)(2,1)} %get-tuple-element.20.dh_ref, f32[4096,1792]{1,0:T(8,128)} %get-tuple-element.21.g_ref, f32[4096,1792]{1,0:T(8,128)} %get-tuple-element.22.u_ref, ...), custom_call_target="tpu_custom_call" | custom-call | flops 37580963840 | bytes 58720256 | tf_op jit(solution)/shard_map/first_back/pallas_call | solution.py:183
  372.6 0.0 reduce-scatter.7.cloned.1.call-update
  372.6 0.0 reduce-scatter.11.cloned.1.call-start
  372.7 0.7 reduce-scatter.11.cloned.1.call-update
  373.4 0.0 reduce-scatter.15.cloned.1.call-start
  373.4 0.7 reduce-scatter.15.cloned.1.call-update
  374.1 0.0 reduce-scatter.9.cloned.1.call-start
  374.1 0.5 reduce-scatter.9.cloned.1.call-update
  374.7 0.0 reduce-scatter.13.cloned.1.call-start
  374.7 0.7 reduce-scatter.13.cloned.1.call-update
  375.4 0.0 reduce-scatter.17.cloned.1.call-start
  375.5 0.0 copy-start.10
  375.5 0.5 reduce-scatter.17.cloned.1.call-update
  376.0 0.0 copy-start.1
  376.0 0.0 copy-start.9
  376.0 0.0 all-reduce.3.cloned.1.call-start
  376.1 38.6 %reduce-scatter.7.cloned.1.call-done = bf16[80,1792]{1,0:T(8,128)(2,1)} async-done(((bf16[640,1792]{1,0:T(8,128)(2,1)}), bf16[80,1792]{1,0:T(8,128)(2,1)}) %reduce-scatter.7.cloned.1.call-update) | async-done | bytes 286736 | tf_op jit(solution)/shard_map/reduce_scatter | solution.py:147
  414.6 45.2 %reduce-scatter.11.cloned.1.call-done = bf16[80,1792]{1,0:T(8,128)(2,1)} async-done(((bf16[640,1792]{1,0:T(8,128)(2,1)}), bf16[80,1792]{1,0:T(8,128)(2,1)}) %reduce-scatter.11.cloned.1.call-update) | async-done | bytes 286736 | tf_op jit(solution)/shard_map/reduce_scatter | solution.py:147
  459.9 45.2 %reduce-scatter.15.cloned.1.call-done = bf16[224,640]{1,0:T(8,128)(2,1)} async-done(((bf16[1792,640]{1,0:T(8,128)(2,1)}), bf16[224,640]{1,0:T(8,128)(2,1)}) %reduce-scatter.15.cloned.1.call-update) | async-done | bytes 286736 | tf_op jit(solution)/shard_map/reduce_scatter | solution.py:147
  505.1 45.1 %reduce-scatter.9.cloned.1.call-done = bf16[80,1792]{1,0:T(8,128)(2,1)} async-done(((bf16[640,1792]{1,0:T(8,128)(2,1)}), bf16[80,1792]{1,0:T(8,128)(2,1)}) %reduce-scatter.9.cloned.1.call-update) | async-done | bytes 286736 | tf_op jit(solution)/shard_map/reduce_scatter | solution.py:147
  550.2 45.2 %reduce-scatter.13.cloned.1.call-done = bf16[80,1792]{1,0:T(8,128)(2,1)} async-done(((bf16[640,1792]{1,0:T(8,128)(2,1)}), bf16[80,1792]{1,0:T(8,128)(2,1)}) %reduce-scatter.13.cloned.1.call-update) | async-done | bytes 286736 | tf_op jit(solution)/shard_map/reduce_scatter | solution.py:147
  595.4 45.1 %reduce-scatter.17.cloned.1.call-done = bf16[224,640]{1,0:T(8,128)(2,1)} async-done(((bf16[1792,640]{1,0:T(8,128)(2,1)}), bf16[224,640]{1,0:T(8,128)(2,1)}) %reduce-scatter.17.cloned.1.call-update) | async-done | bytes 286736 | tf_op jit(solution)/shard_map/reduce_scatter | solution.py:147
  640.5 0.0 all-reduce.3.cloned.1.call-update
  640.5 77.1 %all-reduce.3.cloned.1.call-done = (bf16[1,80,1792]{2,1,0:T(8,128)(2,1)}, bf16[1,80,1792]{2,1,0:T(8,128)(2,1)}, bf16[1,80,1792]{2,1,0:T(8,128)(2,1)}, bf16[1,80,...) async-done(((bf16[1,80,1792]{2,1,0:T(8,128)(2,1)}, bf16[1,80,1792]{2,1,0:T(8,128)(2,1)}, bf16[1,80,1792]{2,1,0:T(8,128)(2,1)}, ...) | async-done | bytes 1720336 | tf_op jit(solution)/shard_map/psum | solution.py:147
  717.6 0.0 copy-done.10
  717.6 0.0 copy-done.1
  717.6 0.0 copy-done.9
  717.6 0.0 copy-start.4
  717.6 0.0 copy-start.5
  717.6 0.0 copy-start.6
  717.6 0.0 copy-start.7
  717.7 0.0 copy-start.8
  717.7 3.1 fusion.10
  720.8 0.0 copy-done.2
  720.8 0.6 copy-done.8
  721.3 0.2 copy-done.11
  721.5 0.1 copy-done.12
  721.6 4.2 fusion.2
  (9 shorter events, 0.0 us)
Async XLA Ops:
  7.2 2.1 copy-start.3
  7.2 34.4 %all-gather.13.cloned.1.call-start = ((), (), s32[]{:S(2)}) async-start(), calls=%async_computation.12 | async-start | bytes 2580480 | tf_op jit(solution)/shard_map/all_gather | solution.py:144
  9.2 1.1 copy-start
  9.2 63.2 %all-gather.15.cloned.1.call-start = ((), (), s32[]{:S(2)}) async-start(), calls=%async_computation.13 | async-start | bytes 2580480 | tf_op jit(solution)/shard_map/all_gather | solution.py:144
  10.1 93.1 %all-gather.17.cloned.1.call-start = ((), (), s32[]{:S(2)}) async-start(), calls=%async_computation.14 | async-start | bytes 2580480 | tf_op jit(solution)/shard_map/all_gather | solution.py:144
  11.2 134.0 %all-gather.19.cloned.1.call-start = ((), (), s32[]{:S(2)}) async-start(), calls=%async_computation.15 | async-start | bytes 2580480 | tf_op jit(solution)/shard_map/all_gather | solution.py:144
  11.8 152.8 %all-gather.21.cloned.1.call-start = ((), (), s32[]{:S(2)}) async-start(), calls=%async_computation.16 | async-start | bytes 2580480 | tf_op jit(solution)/shard_map/all_gather | solution.py:144
  12.4 182.9 %all-gather.23.cloned.1.call-start = ((), (), s32[]{:S(2)}) async-start(), calls=%async_computation.17 | async-start | bytes 2580480 | tf_op jit(solution)/shard_map/all_gather | solution.py:144
  12.9 401.7 %reduce-scatter.7.cloned.1.call-start = ((), (), s32[]{:S(2)}) async-start(), calls=%async_computation.6 | async-start | bytes 2580480 | tf_op jit(solution)/shard_map/reduce_scatter | solution.py:147
  372.6 87.2 %reduce-scatter.11.cloned.1.call-start = ((), (), s32[]{:S(2)}) async-start(), calls=%async_computation.8 | async-start | bytes 2580480 | tf_op jit(solution)/shard_map/reduce_scatter | solution.py:147
  373.4 131.7 %reduce-scatter.15.cloned.1.call-start = ((), (), s32[]{:S(2)}) async-start(), calls=%async_computation.10 | async-start | bytes 2580480 | tf_op jit(solution)/shard_map/reduce_scatter | solution.py:147
  374.1 176.1 %reduce-scatter.9.cloned.1.call-start = ((), (), s32[]{:S(2)}) async-start(), calls=%async_computation.7 | async-start | bytes 2580480 | tf_op jit(solution)/shard_map/reduce_scatter | solution.py:147
  374.7 220.7 %reduce-scatter.13.cloned.1.call-start = ((), (), s32[]{:S(2)}) async-start(), calls=%async_computation.9 | async-start | bytes 2580480 | tf_op jit(solution)/shard_map/reduce_scatter | solution.py:147
  375.4 265.1 %reduce-scatter.17.cloned.1.call-start = ((), (), s32[]{:S(2)}) async-start(), calls=%async_computation.11 | async-start | bytes 2580480 | tf_op jit(solution)/shard_map/reduce_scatter | solution.py:147
  375.5 342.1 %copy-start.10 = (f32[2,224,640]{2,1,0:T(8,128)S(1)}, f32[2,224,640]{2,1,0:T(8,128)}, u32[]{:S(2)}) copy-start(f32[2,224,640]{2,1,0:T(8,128)} %param.18) | copy-start | bytes 3440644
  376.0 341.6 %copy-start.1 = (bf16[2,224,640]{2,1,0:T(8,128)(2,1)S(1)}, bf16[2,224,640]{2,1,0:T(8,128)(2,1)}, u32[]{:S(2)}) copy-start(bf16[2,224,640]{2,1,0:T(8,128)(2,1)} %param.15) | copy-start | bytes 1720324
  376.0 341.6 %copy-start.9 = (f32[2,224,640]{2,1,0:T(8,128)S(1)}, f32[2,224,640]{2,1,0:T(8,128)}, u32[]{:S(2)}) copy-start(f32[2,224,640]{2,1,0:T(8,128)} %param.21) | copy-start | bytes 3440644
  376.0 341.6 %all-reduce.3.cloned.1.call-start = ((), (), s32[]{:S(2)}) async-start(), calls=%async_computation.18 | async-start | bytes 3440640 | tf_op jit(solution)/shard_map/psum | solution.py:147
  717.6 3.2 copy-start.2
  717.6 3.1 copy-start.4
  717.6 3.1 copy-start.5
  717.6 3.1 copy-start.6
  717.6 3.1 copy-start.7
  717.7 3.7 copy-start.8
  717.7 3.8 copy-start.11
  717.7 3.9 copy-start.12
Sparse Core Ops, SparseCore 0:
  10.5 31.0 all-gather.12
  44.0 28.3 all-gather.14
  74.9 28.3 all-gather.16
  105.5 28.3 all-gather.18
  136.2 28.3 all-gather.20
  166.9 28.3 all-gather.22
  372.7 41.8 reduce-scatter.6
  418.0 41.8 reduce-scatter.10
  463.2 41.8 reduce-scatter.14
  508.3 41.8 reduce-scatter.8
  553.5 41.8 reduce-scatter.12
  598.6 41.8 reduce-scatter.16
  643.4 74.1 all-reduce.2

commit v2 on v1

v2 whole, which is shorter than its diff:
```python
import functools

import jax
import jax.numpy as jnp
from jax import lax
from jax.experimental import pallas as pl
from jax.experimental.pallas import tpu as pltpu
from jax.sharding import PartitionSpec as P

F32, BF16 = jnp.float32, jnp.bfloat16
NN = (((1,), (0,)), ((), ()))
NT = (((1,), (1,)), ((), ()))
ANY = pl.BlockSpec(memory_space=pl.ANY)
DMA = pltpu.SemaphoreType.DMA


def dot(a, b, dims=NN):
    return lax.dot_general(a, b, dims, preferred_element_type=F32)


def sigmoid(g):
    return 0.5 * jnp.tanh(0.5 * g) + 0.5


def normed(h):
    wide = h.astype(F32)
    scale = lax.rsqrt(jnp.mean(wide * wide, -1, keepdims=True) + 1e-6)
    return wide, scale


class Place:
    def __init__(self):
        s, z = lax.axis_index("s"), lax.axis_index("r")
        self.s, self.z, self.core, self.chip = s, z, s % 2, s // 2
        self.partner = s + 1 - 2 * self.core
        x, y = self.chip // 2, self.chip % 2
        self.chips = [2 * (x + (1 - 2 * x) * (j // 2)) + (y + (1 - 2 * y) * (j % 2)) for j in range(4)]
        self.peers = [2 * chip + self.core for chip in self.chips]
        self.z_pair = z + 1 - 2 * (z % 2)
        self.inner = (z + 1) // 2 % 2
        self.z_middle = 3 - z

    def barrier(self):
        sem = pltpu.get_barrier_semaphore()
        others = [{"s": self.partner}] + [{"s": p} for p in self.peers[1:]] + [{"r": (self.z + k) % 4} for k in (1, 2, 3)]
        for device in others:
            pl.semaphore_signal(sem, inc=1, device_id=device, device_id_type=pl.DeviceIdType.MESH)
        pl.semaphore_wait(sem, len(others))


def push(src, dst, send, recv, device):
    return pltpu.make_async_remote_copy(
        src_ref=src, dst_ref=dst, send_sem=send, recv_sem=recv, device_id=device, device_id_type=pl.DeviceIdType.MESH
    )


def gather_scratch(n):
    return [DMA((n,))] + [DMA((n, 2))] + [DMA((n, 3, 2))] * 4


class Gather:
    def __init__(self, place, shards, fulls, halved, sems):
        self.p, self.shards, self.fulls, self.halved = place, shards, fulls, halved
        self.own, self.pair, self.ici, self.core, self.along, self.core2 = sems
        self.h = place.z % 2

    def part(self, m, s, h):
        ref, rows = self.fulls[m], self.shards[m].shape[0]
        if not self.halved[m]:
            return ref.at[pl.ds(pl.multiple_of(s * rows, 16), rows)]
        if rows % 32 == 0:
            return ref.at[pl.ds(pl.multiple_of(s * rows + h * (rows // 2), 16), rows // 2)]
        c = ref.shape[1] // 2
        return ref.at[pl.ds(pl.multiple_of(s * rows, 16), rows), pl.ds(pl.multiple_of(h * c, 128), c)]

    def mine(self, m):
        ref, rows, h = self.shards[m], self.shards[m].shape[0], self.h
        if not self.halved[m]:
            return ref
        if rows % 32 == 0:
            return ref.at[pl.ds(pl.multiple_of(h * (rows // 2), 16), rows // 2)]
        c = ref.shape[1] // 2
        return ref.at[:, pl.ds(pl.multiple_of(h * c, 128), c)]

    def local(self, m):
        rows = self.shards[m].shape[0]
        return pltpu.make_async_copy(self.shards[m], self.fulls[m].at[pl.ds(pl.multiple_of(self.p.s * rows, 16), rows)], self.own.at[m])

    def own_rows(self, m, s):
        rows = self.shards[m].shape[0]
        here = self.fulls[m].at[pl.ds(pl.multiple_of(s * rows, 16), rows)]
        return push(self.shards[m], here, self.pair.at[m, 0], self.pair.at[m, 1], {"s": self.p.partner})

    def over_ici(self, m, j, s):
        return push(self.mine(m), self.part(m, s, self.h), self.ici.at[m, j - 1, 0], self.ici.at[m, j - 1, 1], {"s": self.p.peers[j]})

    def to_core(self, m, j, s):
        here = self.part(m, s, self.h)
        return push(here, here, self.core.at[m, j - 1, 0], self.core.at[m, j - 1, 1], {"s": self.p.partner})

    def along_z(self, m, j, h):
        here = self.part(m, self.p.peers[j], h)
        return push(here, here, self.along.at[m, j - 1, 0], self.along.at[m, j - 1, 1], {"r": self.p.z_pair})

    def to_core2(self, m, j, s):
        here = self.part(m, s, 1 - self.h)
        return push(here, here, self.core2.at[m, j - 1, 0], self.core2.at[m, j - 1, 1], {"s": self.p.partner})

    def other(self, j):
        return 2 * self.p.chips[j] + 1 - self.p.core

    def start(self, m):
        for j in (1, 2, 3):
            self.over_ici(m, j, self.p.s).start()
        self.local(m).start()
        self.own_rows(m, self.p.s).start()

    def relay(self, m):
        for j in (1, 2, 3):
            self.over_ici(m, j, self.p.peers[j]).wait_recv()
            if self.halved[m]:
                self.along_z(m, j, self.h).start()
            self.to_core(m, j, self.p.peers[j]).start()

    def relay2(self, m):
        if self.halved[m]:
            for j in (1, 2, 3):
                self.along_z(m, j, 1 - self.h).wait_recv()
                self.to_core2(m, j, self.p.peers[j]).start()

    def finish(self, m):
        self.local(m).wait()
        self.own_rows(m, self.p.partner).wait_recv()
        self.own_rows(m, self.p.s).wait_send()
        for j in (1, 2, 3):
            self.over_ici(m, j, self.p.s).wait_send()
            self.to_core(m, j, self.other(j)).wait_recv()
            self.to_core(m, j, self.p.peers[j]).wait_send()
            if self.halved[m]:
                self.along_z(m, j, self.h).wait_send()
                self.to_core2(m, j, self.other(j)).wait_recv()
                self.to_core2(m, j, self.p.peers[j]).wait_send()


def gather_kernel(*refs, halved):
    n = len(halved)
    shards, fulls, sems = refs[:n], refs[n : 2 * n], refs[2 * n :]
    place = Place()
    place.barrier()
    g = Gather(place, [s.at[0] for s in shards], fulls, halved, sems)
    for stage in (g.start, g.relay, g.relay2, g.finish):
        for m in range(n):
            stage(m)


def reduce_scratch(n, r, c):
    return [
        pltpu.VMEM((n, 4, r, c), BF16),
        pltpu.VMEM((n, 3, r, c), BF16),
        pltpu.VMEM((n, r, c), F32),
        pltpu.VMEM((n, 3, r, c), BF16),
        pltpu.VMEM((n, 2, r, c), BF16),
        pltpu.VMEM((n, 2, r, c), BF16),
        pltpu.VMEM((n, r, c), BF16),
        DMA((n, 2)),
        DMA((n, 3, 2)),
        DMA((n, 3, 2)),
    ]


class Reduce:
    def __init__(self, place, source, own, out, scratch, own_sem=None):
        self.p, self.source, self.own, self.out, self.own_sem = place, source, own, out, own_sem
        self.pair, self.sums, self.kept, self.got, self.sent_z, self.got_z, self.whole, self.s0, self.s1, self.s2 = scratch

    def swap(self, k):
        return push(self.source.at[k, :, 1 - self.p.core], self.pair.at[k], self.s0.at[k, 0], self.s0.at[k, 1], {"s": self.p.partner})

    def load(self, k):
        return pltpu.make_async_copy(self.source.at[k, :, self.p.core], self.own.at[k], self.own_sem.at[k])

    def spread(self, k, j):
        return push(self.sums.at[k, j - 1], self.got.at[k, j - 1], self.s1.at[k, j - 1, 0], self.s1.at[k, j - 1, 1], {"s": self.p.peers[j]})

    def inward(self, k):
        return push(self.sent_z.at[k, 0], self.got_z.at[k, 0], self.s2.at[k, 0, 0], self.s2.at[k, 0, 1], {"r": self.p.z_pair})

    def across(self, k):
        return push(self.sent_z.at[k, 1], self.got_z.at[k, 1], self.s2.at[k, 1, 0], self.s2.at[k, 1, 1], {"r": self.p.z_middle})

    def outward(self, k):
        return push(self.whole.at[k], self.whole.at[k], self.s2.at[k, 2, 0], self.s2.at[k, 2, 1], {"r": self.p.z_pair})

    def at_end(self, f):
        pl.when(self.p.inner == 0)(f)

    def in_middle(self, f):
        pl.when(self.p.inner == 1)(f)

    def stage(self, number, k):
        [self.stage0, self.stage1, self.stage2, self.stage3, self.stage4, self.stage5][number](k)

    def stage0(self, k):
        self.swap(k).start()
        if self.own_sem is not None:
            self.load(k).start()

    def stage1(self, k):
        if self.own_sem is not None:
            self.load(k).wait()
        self.swap(k).wait_recv()
        for j in (3, 1, 2, 0):
            chip = self.p.chips[j]
            mine = self.own[k, chip] if self.own_sem is not None else self.source[k, chip, self.p.core]
            total = mine.astype(F32) + self.pair[k, chip].astype(F32)
            if j:
                self.sums[k, j - 1] = total.astype(BF16)
                self.spread(k, j).start()
            else:
                self.kept[k] = total
        self.swap(k).wait_send()

    def stage2(self, k):
        for j in (1, 2, 3):
            self.spread(k, j).wait()
        total = self.kept[k]
        for j in range(3):
            total = total + self.got[k, j].astype(F32)
        self.kept[k] = total

        @self.at_end
        def _():
            self.sent_z[k, 0] = self.kept[k].astype(BF16)
            self.inward(k).start()

    def stage3(self, k):
        @self.in_middle
        def _():
            self.inward(k).wait_recv()
            self.sent_z[k, 1] = (self.kept[k] + self.got_z[k, 0].astype(F32)).astype(BF16)
            self.across(k).start()

    def stage4(self, k):
        @self.in_middle
        def _():
            self.across(k).wait()
            self.whole[k] = (self.sent_z[k, 1].astype(F32) + self.got_z[k, 1].astype(F32)).astype(BF16)
            self.outward(k).start()

    def stage5(self, k):
        @self.in_middle
        def _():
            self.outward(k).wait_send()

        @self.at_end
        def _():
            self.inward(k).wait_send()
            self.outward(k).wait_recv()

        self.out[k] = self.whole[k]

    def ticks(self, step, offsets, n):
        for t in (1, 5, 4, 3, 2):
            k = step - offsets[t]

            @pl.when((k >= 0) & (k < n))
            def _(k=k, t=t):
                self.stage(t, jnp.clip(k, 0, n - 1))


def first_forward(x_ref, wg_ref, wu_ref, wd_ref, *refs, cut, halved):
    n = len(halved)
    shards, refs = refs[:n], refs[n:]
    h_ref, g_ref, u_ref, at_ref = refs[:4]
    fulls, hid_ref, sems = refs[4 : 4 + n], refs[4 + n], refs[5 + n :]
    i = pl.program_id(0)
    place = Place()
    gather = Gather(place, [s.at[1] for s in shards], fulls, halved, sems)

    @pl.when(i == 0)
    def _():
        place.barrier()
        for m in range(n):
            gather.start(m)

    for m in range(n):
        pl.when(i == 2 + m)(functools.partial(gather.relay, m))
        pl.when(i == 4 + m + m // 2)(functools.partial(gather.relay2, m))

    wide, scale = normed(x_ref[...])
    a = (wide * scale).astype(BF16)
    at_ref[...] = a.T
    ff = wg_ref.shape[1]
    for j in range(0, ff, cut):
        g = dot(a, wg_ref[:, j : j + cut])
        u = dot(a, wu_ref[:, j : j + cut])
        g_ref[:, j : j + cut] = g
        u_ref[:, j : j + cut] = u
        hid_ref[:, j : j + cut] = (g * sigmoid(g) * u).astype(BF16)
    h_ref[...] = x_ref[...] + dot(hid_ref[...], wd_ref[...]).astype(BF16)

    @pl.when(i == pl.num_programs(0) - 1)
    def _():
        for m in range(n):
            gather.finish(m)


def swiglu_back(g, u, dhid):
    dhid = dhid.astype(BF16).astype(F32)
    sig = sigmoid(g)
    s = g * sig
    return (s * u).astype(BF16), (dhid * u * (sig * (1.0 + g - s))).astype(BF16), (dhid * s).astype(BF16)


def last_layer(h_ref, dy_ref, wg_ref, wu_ref, wd_ref, dh_ref, at_ref, dg_ref, du_ref, od_ref, acc_d, *, cut):
    i, n = pl.program_id(0), pl.num_programs(0)

    @pl.when(i == 0)
    def _():
        acc_d[...] = jnp.zeros_like(acc_d)

    wide, scale = normed(h_ref[...])
    a = (wide * scale).astype(BF16)
    at_ref[...] = a.T
    dy = dy_ref[...]
    dy_t = dy.T
    ff = wg_ref.shape[1]
    for j in range(0, ff, cut):
        at = slice(j, j + cut)
        g = dot(a, wg_ref[:, at])
        u = dot(a, wu_ref[:, at])
        hid, dg, du = swiglu_back(g, u, dot(dy, wd_ref[at, :], NT))
        dg_ref[:, at] = dg
        du_ref[:, at] = du
        acc_d[:, at] += dot(dy_t, hid)
    da = (dot(dg_ref[...], wg_ref[...], NT) + dot(du_ref[...], wu_ref[...], NT)).astype(BF16).astype(F32)
    inner = jnp.mean(da * wide, -1, keepdims=True)
    by_norm = scale * da - wide * (scale * scale * scale * inner)
    dh_ref[...] = dy + by_norm.astype(BF16)

    @pl.when(i == n - 1)
    def _():
        od_ref[...] = acc_d[...].T.astype(BF16)


def first_back(dh_ref, g_ref, u_ref, wd_ref, source, dg_ref, du_ref, od_ref, gu_ref, acc_d, own, own_sem, *scratch, cut, chunks):
    i, n = pl.program_id(0), pl.num_programs(0)
    place = Place()
    first, count = chunks
    reduce = Reduce(place, source.at[pl.ds(first, count)], own, gu_ref, scratch, own_sem)
    offsets = [0, 1, 3, 4, 5, 6]

    @pl.when(i == 0)
    def _():
        acc_d[...] = jnp.zeros_like(acc_d)
        place.barrier()
        for k in range(count):
            reduce.stage0(k)

    reduce.ticks(i, offsets, count)
    dh = dh_ref[...]
    dh_t = dh.T
    ff = g_ref.shape[1]
    for j in range(0, ff, cut):
        at = slice(j, j + cut)
        hid, dg, du = swiglu_back(g_ref[:, at], u_ref[:, at], dot(dh, wd_ref[at, :], NT))
        dg_ref[:, at] = dg
        du_ref[:, at] = du
        acc_d[:, at] += dot(dh_t, hid)

    @pl.when(i == n - 1)
    def _():
        od_ref[...] = acc_d[...].T.astype(BF16)

        @pl.loop(n, max(n, count + offsets[-1]))
        def _(step):
            reduce.ticks(step, offsets, count)


def by_weights(at_ref, dg_ref, du_ref, dsource, *refs, count, total):
    some = total > count
    if some:
        left_ref, refs = refs[0], refs[1:]
    gu_ref, d_ref, chunk, down_own, down_sem = refs[:5]
    i = pl.program_id(0)
    place = Place()
    down = Reduce(place, dsource, down_own, d_ref, refs[5:15], down_sem)
    gu = Reduce(place, chunk, None, gu_ref, refs[15:])
    down_offsets, gu_offsets = [0, 1, 5, 7, 8, 10], [0, 1, 5, 6, 7, 8]

    @pl.when(i == 0)
    def _():
        place.barrier()
        down.stage0(0)

    def ticks(step):
        down.ticks(step, down_offsets, 1)
        gu.ticks(step, gu_offsets, count)

    ticks(i)
    for half, ref in enumerate((dg_ref, du_ref)):
        block = dot(at_ref[...], ref[...]).astype(BF16)
        rows = block.shape[0] // 8
        for s in range(8):
            to = slice(half * rows, (half + 1) * rows)
            if some:
                left_ref[0, s // 2, s % 2, to] = block[s * rows : (s + 1) * rows]
            else:
                chunk[i, s // 2, s % 2, to] = block[s * rows : (s + 1) * rows]
    if some:

        @pl.when(i < count)
        def _():
            chunk[jnp.clip(i, 0, count - 1)] = left_ref[0]

    @pl.when(i < count)
    def _():
        gu.stage0(jnp.clip(i, 0, count - 1))

    @pl.when(i == total - 1)
    def _():
        @pl.loop(total, max(total, down_offsets[-1] + 1, count + gu_offsets[-1]))
        def _(step):
            ticks(step)


def whole(shape):
    return pl.BlockSpec(shape, lambda i: (0,) * len(shape), pipeline_mode=pl.Buffered(1))


def rows(n, width):
    return pl.BlockSpec((n, width), lambda i: (i, 0))


def columns(height, n):
    return pl.BlockSpec((height, n), lambda i: (0, i))


def struct(shape, dtype=BF16):
    return jax.ShapeDtypeStruct(shape, dtype)


def params(number=None, mib=62):
    extra = {} if number is None else {"collective_id": number, "has_side_effects": True}
    return pltpu.CompilerParams(vmem_limit_bytes=mib * 2**20, dimension_semantics=("arbitrary",), **extra)


def adamw(w, m, v, g):
    m = 0.9 * m + 0.1 * g
    v = 0.95 * v + 0.05 * g * g
    step = m * lax.rsqrt(v + 1e-8) + 0.1 * w
    return (w - 0.02 * step).astype(BF16), m, v


def solution(mesh):
    early = 2

    def step(x, dy, *arrays):
        weights, m, v = (arrays[i : i + 3] for i in (0, 3, 6))
        x, dy = x[0], dy[0]
        tokens, d = x.shape
        ff = weights[0].shape[2]
        cut, tile = 256, 512
        n, many = tokens // tile, ff // cut
        fulls = [struct((d, ff)), struct((d, ff)), struct((ff, d))]
        blocks = (d // 4, cut)
        down_blocks = (ff // 8, d)
        wide = struct((tokens, ff))

        by0 = pl.pallas_call(
            functools.partial(gather_kernel, halved=(True, True, False)),
            in_specs=[ANY] * 3,
            out_specs=[ANY] * 3,
            out_shape=fulls,
            scratch_shapes=gather_scratch(3),
            compiler_params=pltpu.CompilerParams(collective_id=0, has_side_effects=True),
            name="gather_first",
        )(*weights)

        h, g, u, a0_t, *by1 = pl.pallas_call(
            functools.partial(first_forward, cut=cut, halved=(True, True, True)),
            grid=(n,),
            in_specs=[rows(tile, d), whole((d, ff)), whole((d, ff)), whole((ff, d))] + [ANY] * 3,
            out_specs=[rows(tile, d), rows(tile, ff), rows(tile, ff), columns(d, tile)] + [ANY] * 3,
            out_shape=[struct((tokens, d)), struct((tokens, ff), F32), struct((tokens, ff), F32), struct((d, tokens))] + fulls,
            scratch_shapes=[pltpu.VMEM((tile, ff), BF16)] + gather_scratch(3),
            compiler_params=params(1),
            name="first_forward",
        )(x, *by0, *weights)

        dh, a1_t, dg1, du1, by_d1 = pl.pallas_call(
            functools.partial(last_layer, cut=cut),
            grid=(n,),
            in_specs=[rows(tile, d), rows(tile, d), whole((d, ff)), whole((d, ff)), whole((ff, d))],
            out_specs=[rows(tile, d), columns(d, tile), rows(tile, ff), rows(tile, ff), whole((ff, d))],
            out_shape=[struct((tokens, d)), struct((d, tokens)), wide, wide, struct((ff, d))],
            scratch_shapes=[pltpu.VMEM((d, ff), F32)],
            compiler_params=params(),
            name="last_layer",
        )(h, dy, *by1)

        def summed(a_t, dg, du, by_d, count, number):
            some = many > count
            outs = [struct((count,) + blocks), struct((1,) + down_blocks)]
            specs = [whole((count,) + blocks), whole((1,) + down_blocks)]
            if some:
                outs = [struct((many, 4, 2) + blocks)] + outs
                specs = [pl.BlockSpec((1, 4, 2) + blocks, lambda i: (i, 0, 0, 0, 0))] + specs
            return pl.pallas_call(
                functools.partial(by_weights, count=count, total=many),
                grid=(many,),
                in_specs=[whole((d, tokens)), columns(tokens, cut), columns(tokens, cut), ANY],
                out_specs=specs,
                out_shape=outs,
                scratch_shapes=[pltpu.VMEM((count, 4, 2) + blocks, BF16), pltpu.VMEM((1, 4) + down_blocks, BF16), DMA((1,))]
                + reduce_scratch(1, *down_blocks)
                + reduce_scratch(count, *blocks),
                compiler_params=params(number),
                name=f"by_weights_{number}",
            )(a_t, dg, du, by_d.reshape((1, 4, 2) + down_blocks))

        left, early_gu1, sum_d1 = summed(a1_t, dg1, du1, by_d1, early, 2)

        late = many - early
        dg0, du0, by_d0, late_gu1 = pl.pallas_call(
            functools.partial(first_back, cut=cut, chunks=(early, late)),
            grid=(n,),
            in_specs=[rows(tile, d), rows(tile, ff), rows(tile, ff), whole((ff, d)), ANY],
            out_specs=[rows(tile, ff), rows(tile, ff), whole((ff, d)), whole((late,) + blocks)],
            out_shape=[wide, wide, struct((ff, d)), struct((late,) + blocks)],
            scratch_shapes=[pltpu.VMEM((d, ff), F32), pltpu.VMEM((late, 4) + blocks, BF16), DMA((late,))] + reduce_scratch(late, *blocks),
            compiler_params=params(3),
            name="first_back",
        )(dh, g, u, by0[2], left)

        gu0, sum_d0 = summed(a0_t, dg0, du0, by_d0, many, 4)
        gu = jnp.stack([gu0, jnp.concatenate([early_gu1, late_gu1])])
        gu = gu.reshape(2, many, 2, d // 8, cut).transpose(2, 0, 3, 1, 4).reshape(2, 2, d // 8, ff)
        gradients = [gu[0], gu[1], jnp.concatenate([sum_d0, sum_d1])]
        new = [adamw(w.astype(F32), mm, vv, gg.astype(F32)) for w, mm, vv, gg in zip(weights, m, v, gradients, strict=True)]
        return tuple(one[which] for which in range(3) for one in new)

    states, cut = P(("rep", "r", "s"), None, None), P(None, "s", None)
    return jax.shard_map(
        step,
        mesh=mesh,
        in_specs=(states, states) + (cut,) * 9,
        out_specs=(P("rep", "s", None),) * 9,
        check_vma=False,
    )
```

time: 733 us -> 382 us (0.52)
  waiting for transfers between devices: 487 us -> 0 us
  Pallas kernels: 219 us -> 367 us
  between operations: 14 us -> 0.8 us
    reduce_scatter x6 -> x0, waiting for transfers between devices: 264 us -> none  [summed(): lax.psum_scatter(term, 's', scatter_dimension=0, tiled=True)]
    pallas_call x3 -> x6, Pallas kernels: 219 us -> 367 us  [the longest x2 131 us: summed(): pl.pallas_call(functools.partial(by_weights, count=count, total=many), gr...]
    all_gather x6 -> x0, waiting for transfers between devices: 140 us -> none  [fetched(): return [lax.all_gather(w[number], 's', axis=0, tiled=True) for w in weights]]
    psum x1 -> x0, waiting for transfers between devices: 77.1 us -> none  [summed(): lax.psum(lax.psum_scatter(term, 's', scatter_dimension=0, tiled=True), 'r')]
  transfers between devices with their start and end apart: 13 -> 0, of which waited for: 12 -> 0; matrix products, arithmetic and copies ran while one was open for 0% -> 0% of each run, Pallas kernels for 6% -> 0%
where the time goes in v2:
time: 382 us; the launch traced here: 381 us
  Pallas kernels  367 us (96%)
  other arithmetic  8.65 us (2%)
  local copies, waits for them, and re-layouts  4.9 us (1%)
    pallas_call x2, Pallas kernels, summed(): pl.pallas_call(functools.partial(by_weights, count=count, total=many), gr...  131 us
    pallas_call x1, Pallas kernels, step(): pl.pallas_call(functools.partial(last_layer, cut=cut), grid=(n,), in_spec...  95.1 us
    pallas_call x1, Pallas kernels, step(): pl.pallas_call(functools.partial(first_forward, cut=cut, halved=(True, Tr...  53.9 us
    pallas_call x1, Pallas kernels, step(): pl.pallas_call(functools.partial(first_back, cut=cut, chunks=(early, late...  51.4 us
    pallas_call x1, Pallas kernels, step(): pl.pallas_call(functools.partial(gather_kernel, halved=(True, True, False...  36 us
    convert_element_type x2, other arithmetic, adamw(): return ((w - 0.02 * step).astype(BF16), m, v)  8.08 us

profile of v2, /device:TPU:0, one launch (start us, length us, event | category | flops | bytes accessed | tf_op | source)
XLA Modules:
  0.0 381.3 jit_solution(8482693085898828603)
XLA Ops:
  0.6 36.0 %gather_first.1 = (bf16[640,1792]{1,0:T(8,128)(2,1)}, bf16[640,1792]{1,0:T(8,128)(2,1)}, bf16[1792,640]{1,0:T(8,128)(2,1)}) custom-call(bf16[2,80,1792]{2,1,0:T(8,128)(2,1)} %refs_0_.3, bf16[2,80,1792]{2,1,0:T(8,128)(2,1)} %refs_1_.3, bf16[2,224,640]{2,1,0:T(8,128)(2,1)} %refs_2_.3), custom_call_target="tpu_custom_call" | custom-call | tf_op jit(solution)/shard_map/gather_first/pallas_call | solution.py:470
  36.7 53.9 %first_forward.1 = (bf16[4096,640]{1,0:T(8,128)(2,1)}, f32[4096,1792]{1,0:T(8,128)}, f32[4096,1792]{1,0:T(8,128)}, bf16[640,4096]{1,0:T(8,128)(2,1)}, bf16[640,1...) custom-call(bf16[4096,640]{1,0:T(8,128)(2,1)} %bitcast.8, ...), custom_call_target="tpu_custom_call" | custom-call | tf_op jit(solution)/shard_map/first_forward/pallas_call | solution.py:480
  90.6 95.1 %last_layer.1 = (bf16[4096,640]{1,0:T(8,128)(2,1)}, bf16[640,4096]{1,0:T(8,128)(2,1)}, bf16[4096,1792]{1,0:T(8,128)(2,1)}, bf16[4096,1792]{1,0:T(8,128)(2,1)}, bf16[1792,640]{1,0:T(8,128)(2,1)}) custom-call(bf16[4096,640]{1,0:T(8,128)(2,1)} %get-tuple-element.37.h_ref, bf16[4096,640]{1,0:T(8,128)(2,1)} %bitcast.9, ...), custom_call_target="tpu_custom_call" | custom-call | tf_op jit(solution)/shard_map/last_layer/pallas_call | solution.py:491
  185.7 54.0 %by_weights_2.1 = (bf16[7,4,2,160,256]{4,3,2,1,0:T(8,128)(2,1)}, bf16[2,160,256]{2,1,0:T(8,128)(2,1)}, bf16[1,224,640]{2,1,0:T(8,128)(2,1)}) custom-call(bf16[640,4096]{1,0:T(8,128)(2,1)} %get-tuple-element.44.at_ref, bf16[4096,1792]{1,0:T(8,128)(2,1)} %get-tuple-element.45.dg_ref, bf16[4096,1792]{1,0:T(8,128)(2,1)} %get-tuple-element.46.du_ref, ...), custom_call_target="tpu_custom_call" | custom-call | tf_op jit(solution)/shard_map/by_weights_2/pallas_call | solution.py:509
  239.7 51.4 %first_back.1 = (bf16[4096,1792]{1,0:T(8,128)(2,1)}, bf16[4096,1792]{1,0:T(8,128)(2,1)}, bf16[1792,640]{1,0:T(8,128)(2,1)}, bf16[5,160,256]{2,1,0:T(8,128)(2,1)}) custom-call(bf16[4096,640]{1,0:T(8,128)(2,1)} %get-tuple-element.41.dh_ref, f32[4096,1792]{1,0:T(8,128)} %get-tuple-element.42.g_ref, f32[4096,1792]{1,0:T(8,128)} %get-tuple-element.43.u_ref, ...), custom_call_target="tpu_custom_call" | custom-call | tf_op jit(solution)/shard_map/first_back/pallas_call | solution.py:525
  291.0 76.6 %by_weights_4.1 = (bf16[7,160,256]{2,1,0:T(8,128)(2,1)}, bf16[1,224,640]{2,1,0:T(8,128)(2,1)}) custom-call(bf16[640,4096]{1,0:T(8,128)(2,1)} %get-tuple-element.36.at_ref, bf16[4096,1792]{1,0:T(8,128)(2,1)} %get-tuple-element.49.dg_ref, bf16[4096,1792]{1,0:T(8,128)(2,1)} %get-tuple-element.50.du_ref, bf16[1,4,2,224,640]{4,3,2,1,0:T(8,128)(2,1)} %bitcast.11), custom_call_target="tpu_custom_call" | custom-call | tf_op jit(solution)/shard_map/by_weights_4/pallas_call | solution.py:509
  367.7 0.0 copy-start.7
  367.7 0.0 copy-start.9
  367.7 1.4 copy.22
  369.1 0.0 copy-done.7
  369.1 0.0 copy-done.9
  369.1 0.1 pad_maximum_fusion
  369.2 0.3 copy.23
  369.5 0.3 maximum_bitcast_fusion
  369.8 0.2 slice_convert_fusion
  370.1 1.4 reshape.41
  371.5 0.0 copy-start
  371.5 0.0 copy-start.8
  371.5 0.4 reshape.40
  371.9 0.7 copy-done
  372.5 0.1 copy-done.8
  372.6 0.0 copy-start.1
  372.6 0.0 copy-start.2
  372.6 0.0 copy-start.3
  372.6 0.0 copy-start.4
  372.6 0.0 copy-start.5
  372.6 0.0 copy-start.6
  372.6 3.7 fusion.8
  376.3 0.0 copy-done.1
  376.3 0.0 copy-done.2
  376.3 0.0 copy-done.3
  376.3 0.0 copy-done.4
  376.4 0.0 copy-done.5
  376.4 0.6 copy-done.6
  376.9 4.4 %fusion.2 = (bf16[2,80,1792]{2,1,0:T(8,128)(2,1)}, f32[2,80,1792]{2,1,0:T(8,128)}, f32[2,80,1792]{2,1,0:T(8,128)}, bf16[2,80,1792]{2,1,0:T(8,128)(2,1)}, f32[2,80,1792]{2,1,0:T(8,128)}, /*index=5*/f32[2,80,1792]{2,1,0:T(8,128)}) fusion(bf16[2,80,1792]{2,1,0:T(8,128)(2,1)S(1)} %copy-done.1, f32[2,80,1792]{2,1,0:T(8,128)S(1)} %reshape.40, ...), kind=kLoop, calls=%fused_computation.13 | loop fusion | flops 8601600 | bytes 13762560 | tf_op jit(solution)/shard_map/convert_element_type | solution.py:452
Async XLA Ops:
  367.7 1.5 copy-start.7
  367.7 1.5 copy-start.9
  371.5 1.1 copy-start
  371.5 1.1 copy-start.8
  372.6 3.7 copy-start.1
  372.6 3.7 copy-start.2
  372.6 3.7 copy-start.3
  372.6 3.7 copy-start.4
  372.6 3.8 copy-start.5
  372.6 4.3 %copy-start.6 = (f32[2,80,1792]{2,1,0:T(8,128)S(1)}, f32[2,80,1792]{2,1,0:T(8,128)}, u32[]{:S(2)}) copy-start(f32[2,80,1792]{2,1,0:T(8,128)} %param.20) | copy-start | bytes 3440644
